TPU v7x, 256 devices: a whole 4x4x8 slice. The times are simulated.
256 devices in a mesh: ta: 64 (over y, z_hi, x, core), ga: 4 (over z_lo).
Axes of the slice: x: 4, y: 4, z: 8 (z_hi: 2, z_lo: 4; z = z_hi * 4 + z_lo), core: 2. Of those that a mesh axis runs over, the one named last changes fastest.
Arguments:
- snapshots: bfloat16 [1024, 4, 131072], P('ta', 'ga'), may hold values from -12 to 12
- block_starts: int32 [7], replicated, may hold values from 0 to 768
- kept_freqs: int32 [32], replicated, may hold values from 0 to 128
Outputs:
- spectra: bfloat16 [4, 7, 2, 32, 131072], P('ga', None, None, None, 'ta')
- power_step: float32 [4, 7, 2, 32, 131072], P('ga', None, None, None, 'ta')
All inputs are finite; a program needn't handle non-finite values.
Results may differ from a plain program's by a relative error of at most 0.0047.
Values may be sent and summed in bfloat16 or wider, within the bound.
No kernel may reach another device: no remote copies, remote signals or barrier semaphores. Data moves between devices by JAX's collectives and lax.ppermute only.
A program may use at most 192 MiB of HBM per device.

v0:
```python
import math

import jax
import jax.numpy as jnp
from jax import lax
from jax.sharding import Mesh
from jax.sharding import PartitionSpec as P

NFFT = 256
NB = 7
NF = 32
TA = ("ta_0", "ta_1", "ta_2", "ta_3")
TA_GA = ("ta_0", "ta_1", "ta_2", "ta_3", "ga")


def one_axis_at_a_time(x, axes):
    for axis in axes:
        x = lax.psum(x, axis)
    return x


def kernel_table(kept_freqs, sample_index):
    phase_index = kept_freqs[:, None] * sample_index[None, :] % NFFT
    angle_val = 2.0 * math.pi / NFFT * phase_index.astype(jnp.float32)
    window = 0.5 - 0.5 * jnp.cos(2.0 * math.pi / NFFT * sample_index.astype(jnp.float32))
    norm_scale = 2.0 / math.sqrt(NFFT)
    real_rows = window[None, :] * jnp.cos(angle_val) * norm_scale
    imag_rows = -window[None, :] * jnp.sin(angle_val) * norm_scale
    return jnp.concatenate([real_rows, imag_rows], axis=0)


def transform(series, kernel_rows, block_starts):
    blocks = []
    for block_index in range(NB):
        segment = lax.dynamic_slice_in_dim(series, block_starts[block_index], NFFT, 0)
        blocks.append(jnp.dot(kernel_rows, segment, preferred_element_type=jnp.float32))
    return jnp.stack(blocks).astype(jnp.bfloat16)


def gram_terms(spectra):
    values = spectra.reshape(NB, 2, NF, -1)
    real_part = values[:, 0]
    imag_part = values[:, 1]
    f32 = jnp.float32
    gram_re = jnp.einsum(
        "bfp,cfp->fbc", real_part, real_part, preferred_element_type=f32
    ) + jnp.einsum("bfp,cfp->fbc", imag_part, imag_part, preferred_element_type=f32)
    gram_im = jnp.einsum(
        "bfp,cfp->fbc", real_part, imag_part, preferred_element_type=f32
    ) - jnp.einsum("bfp,cfp->fbc", imag_part, real_part, preferred_element_type=f32)
    return (gram_re, gram_im)


def power_apply(spectra, gram_re, gram_im):
    values = spectra.astype(jnp.float32).reshape(NB, 2, NF, -1)
    real_part = values[:, 0]
    imag_part = values[:, 1]
    out_re = jnp.einsum("cfp,fcb->bfp", real_part, gram_re) - jnp.einsum(
        "cfp,fcb->bfp", imag_part, gram_im
    )
    out_im = jnp.einsum("cfp,fcb->bfp", real_part, gram_im) + jnp.einsum(
        "cfp,fcb->bfp", imag_part, gram_re
    )
    return jnp.stack([out_re, out_im], axis=1)


def shards(snapshots, block_starts, kept_freqs):
    ta_count = lax.axis_size(TA)
    ga_count = lax.axis_size("ga")
    local_times = snapshots.shape[0]
    own_pts = snapshots.shape[2] // ta_count
    all_times = local_times * ta_count
    kernel_rows = kernel_table(kept_freqs, jnp.arange(NFFT, dtype=jnp.int32)).astype(jnp.bfloat16)
    shaped = snapshots.reshape(local_times, ta_count, own_pts)
    zero_gram = jnp.zeros((NF, NB, NB), jnp.float32)
    early_sums = (zero_gram, zero_gram)
    arrived = lax.all_to_all(shaped, TA, split_axis=1, concat_axis=0, tiled=True)
    spectra = transform(arrived.reshape(all_times, own_pts), kernel_rows, block_starts)
    late_sums = gram_terms(spectra)
    summed = (one_axis_at_a_time(late_sums[0], TA_GA), one_axis_at_a_time(late_sums[1], TA_GA))
    denominator = float(NB * own_pts * ta_count * ga_count)
    gram_re = summed[0] / denominator
    gram_im = summed[1] / denominator
    power = power_apply(spectra, gram_re, gram_im)
    return (spectra.reshape(1, NB, 2, NF, own_pts), power.reshape(1, NB, 2, NF, own_pts))


def solution(mesh):
    split = Mesh(
        mesh.devices.reshape(4, 2, 4, 2, mesh.shape["ga"]), ("ta_0", "ta_1", "ta_2", "ta_3", "ga")
    )
    placed = (P(TA, "ga", None), P(), P())
    return jax.shard_map(
        shards,
        mesh=split,
        in_specs=placed,
        out_specs=(P("ga", None, None, None, TA), P("ga", None, None, None, TA)),
        check_vma=False,
    )
```

profile of v0, /device:TPU:1, one launch (start us, length us, event | category | flops | bytes accessed | tf_op | source)
XLA Modules:
  0.0 238.6 jit_solution(3636419704104790843)
XLA Ops:
  0.6 4.5 %copy.72 = bf16[2,8,64,2048]{3,2,1,0:T(8,128)(2,1)S(1)} copy(bf16[2,8,64,2048]{3,1,2,0:T(8,128)(2,1)} %bitcast.59) | data formatting | bytes 8388608
  5.1 4.3 %copy.55 = bf16[16,64,2048]{2,0,1:T(8,128)(2,1)} copy(bf16[16,64,2048]{2,1,0:T(8,128)(2,1)S(1)} %bitcast.58) | data formatting | bytes 8388608 | tf_op jit(solution)/shard_map/reshape | solution.py:74
  9.4 15.9 %all-to-all-start = ((bf16[16,64,2048]{2,0,1:T(8,128)(2,1)}), bf16[16,64,2048]{2,0,1:T(8,128)(2,1)}, u32[]{:S(2)}, u32[]{:S(2)}) async-start(bf16[16,64,2048]{2,0,1:T(8,128)(2,1)} %copy.55), calls=%async_computation | async-start | bytes 8388608 | tf_op jit(solution)/shard_map/all_to_all | solution.py:77
  39.3 68.2 %all-to-all-done = bf16[16,64,2048]{2,0,1:T(8,128)(2,1)} async-done(((bf16[16,64,2048]{2,0,1:T(8,128)(2,1)}), bf16[16,64,2048]{2,0,1:T(8,128)(2,1)}, u32[]{:S(2)}, u32[]{:S(2)}) %all-to-all-start) | async-done | bytes 4194336 | tf_op jit(solution)/shard_map/all_to_all | solution.py:77
  107.4 1.6 convolution_convert_fusion
  109.1 1.7 convolution_convert_fusion.1
  110.7 1.7 convolution_convert_fusion.2
  112.4 1.6 convolution_convert_fusion.3
  114.0 1.7 convolution_convert_fusion.4
  115.7 1.7 convolution_convert_fusion.5
  117.4 1.7 convolution_convert_fusion.6
  119.1 1.2 copy.57
  120.3 1.2 copy.56
  121.5 1.2 copy.58
  122.7 1.2 copy.59
  123.9 1.2 copy.60
  125.1 1.2 copy.61
  126.3 1.2 copy.62
  127.5 9.9 %stack.64 = bf16[7,2,32,2048]{3,0,2,1:T(8,128)(2,1)S(1)} concatenate(bf16[1,2,32,2048]{3,0,2,1:T(2,128)(2,1)} %copy.56, bf16[1,2,32,2048]{3,0,2,1:T(2,128)(2,1)} %copy.57, bf16[1,2,32,2048]{3,0,2,1:T(2,128)(2,1)} %copy.58, bf16[1,2,32,2048]{3,0,2,1:T(2,128)(2,1)} %copy.59, bf16[1,2,32,2048]{3,0,2,1:T(2,128)(2,1)} %copy.60, bf16[1,2,32,2048]{3,0,2,1:T(2,128)(2,1)} %copy.61, ...), dimensions={0} | concatenate | bytes 3670016 | tf_op jit(solution)/shard_map/stack | solution.py:37
  137.5 1.4 fusion.11
  138.9 1.4 fusion.10
  140.3 1.4 fusion.14
  142.5 1.6 copy.66
  144.1 1.6 copy.67
  145.7 1.6 copy.64
  149.6 27.9 %all-reduce.2 = (f32[32,7,7]{0,2,1:T(8,128)S(1)}, f32[32,7,7]{0,2,1:T(8,128)S(1)}) all-reduce(f32[32,7,7]{0,2,1:T(8,128)S(1)} %sub.22, f32[32,7,7]{0,2,1:T(8,128)S(1)} %add.64), channel_id=1, replica_groups=mesh['ta_0'=4,'ta_1'=2,'ta_2'=4,'ta_3'=2,'ga'=4] {'ta_0'}, use_global_device_ids=true, to_apply=%region_5.6 | all-reduce | flops 3136 | bytes 25088 | tf_op jit(solution)/shard_map/psum | solution.py:18
  177.6 11.9 %all-reduce.4 = (f32[32,7,7]{0,2,1:T(8,128)S(1)}, f32[32,7,7]{0,2,1:T(8,128)S(1)}) all-reduce(f32[32,7,7]{0,2,1:T(8,128)S(1)} %get-tuple-element.16, f32[32,7,7]{0,2,1:T(8,128)S(1)} %get-tuple-element.17), channel_id=1, replica_groups=mesh['ta_0'=4,'ta_1'=2,'ta_2'=4,'ta_3'=2,'ga'=4] {'ta_1'}, use_global_device_ids=true, to_apply=%region_6.7 | all-reduce | flops 3136 | bytes 25088 | tf_op jit(solution)/shard_map/psum | solution.py:18
  189.4 11.4 %all-reduce.1 = (f32[32,7,7]{0,2,1:T(8,128)S(1)}, f32[32,7,7]{0,2,1:T(8,128)S(1)}) all-reduce(f32[32,7,7]{0,2,1:T(8,128)S(1)} %get-tuple-element.20, f32[32,7,7]{0,2,1:T(8,128)S(1)} %get-tuple-element.21), channel_id=1, replica_groups=mesh['ta_0'=4,'ta_1'=2,'ta_2'=4,'ta_3'=2,'ga'=4] {'ta_2'}, use_global_device_ids=true, to_apply=%region_7.8 | all-reduce | flops 3136 | bytes 25088 | tf_op jit(solution)/shard_map/psum | solution.py:18
  200.8 11.3 %all-reduce.3 = (f32[32,7,7]{0,2,1:T(8,128)S(1)}, f32[32,7,7]{0,2,1:T(8,128)S(1)}) all-reduce(f32[32,7,7]{0,2,1:T(8,128)S(1)} %get-tuple-element.14, f32[32,7,7]{0,2,1:T(8,128)S(1)} %get-tuple-element.15), channel_id=1, replica_groups=mesh['ta_0'=4,'ta_1'=2,'ta_2'=4,'ta_3'=2,'ga'=4] {'ta_3'}, use_global_device_ids=true, to_apply=%region_8.9 | all-reduce | flops 3136 | bytes 25088 | tf_op jit(solution)/shard_map/psum | solution.py:18
  212.1 17.3 %all-reduce = (f32[32,7,7]{0,2,1:T(8,128)S(1)}, f32[32,7,7]{0,2,1:T(8,128)S(1)}) all-reduce(f32[32,7,7]{0,2,1:T(8,128)S(1)} %get-tuple-element.18, f32[32,7,7]{0,2,1:T(8,128)S(1)} %get-tuple-element.19), channel_id=1, replica_groups=mesh['ta_0'=4,'ta_1'=2,'ta_2'=4,'ta_3'=2,'ga'=4] {'ga'}, use_global_device_ids=true, to_apply=%region_9.10 | all-reduce | flops 3136 | bytes 25088 | tf_op jit(solution)/shard_map/psum | solution.py:18
  233.2 4.0 %copy.71 = f32[1,7,2,32,2048]{4,3,2,1,0:T(8,128)} copy(f32[1,7,2,32,2048]{4,1,3,2,0:T(8,128)S(1)} %maximum_bitcast_fusion) | data formatting | bytes 7340032
  237.4 1.2 copy-done.3
  (34 shorter events, 7.8 us)
Async XLA Ops:
  9.4 16.0 %copy-start.4 = (s32[7]{0:T(128)S(1)}, s32[7]{0:T(128)}, u32[]{:S(2)}) copy-start(s32[7]{0:T(128)} %param.4) | copy-start | bytes 88
  9.4 29.7 %copy-start.5 = (s32[32]{0:T(128)S(1)}, s32[32]{0:T(128)}, u32[]{:S(2)}) copy-start(s32[32]{0:T(128)} %param.5) | copy-start | bytes 388
  9.4 98.0 %all-to-all-start = ((bf16[16,64,2048]{2,0,1:T(8,128)(2,1)}), bf16[16,64,2048]{2,0,1:T(8,128)(2,1)}, u32[]{:S(2)}, u32[]{:S(2)}) async-start(bf16[16,64,2048]{2,0,1:T(8,128)(2,1)} %copy.55), calls=%async_computation | async-start | bytes 8388608 | tf_op jit(solution)/shard_map/all_to_all | solution.py:77
  117.3 6.5 %copy-start = (bf16[64,2048]{1,0:T(8,128)(2,1)}, bf16[64,2048]{1,0:T(8,128)(2,1)S(1)}, u32[]{:S(2)}) copy-start(bf16[64,2048]{1,0:T(8,128)(2,1)S(1)} %convolution_convert_fusion.5) | copy-start | bytes 786436
  119.1 7.2 %copy-start.2 = (bf16[64,2048]{1,0:T(8,128)(2,1)}, bf16[64,2048]{1,0:T(8,128)(2,1)S(1)}, u32[]{:S(2)}) copy-start(bf16[64,2048]{1,0:T(8,128)(2,1)S(1)} %convolution_convert_fusion.6) | copy-start | bytes 786436
  233.2 4.0 %copy-start.1 = (bf16[64,2048]{1,0:T(8,128)(2,1)S(1)}, bf16[64,2048]{1,0:T(8,128)(2,1)}, u32[]{:S(2)}) copy-start(bf16[64,2048]{1,0:T(8,128)(2,1)} %copy-done) | copy-start | bytes 786436
  237.4 1.2 copy-start.3
where the time goes:
time: 241 us; the launch traced here: 239 us
  blocking collectives  79.8 us (33%)
  waiting for transfers between devices  68.2 us (28%)
  local copies, waits for them, and re-layouts  39.9 us (17%)
  matrix products  18.3 us (8%)
  starting transfers between devices  15.9 us (7%)
  between operations  13.9 us (6%)
  other arithmetic  2.56 us (1%)
    psum x5, blocking collectives, one_axis_at_a_time(): x = lax.psum(x, axis)  79.8 us
    all_to_all x1, waiting for transfers between devices, shards(): lax.all_to_all(shaped, TA, split_axis=1, concat_axis=0, tiled=True)  68.2 us
    another operation x9, local copies, waits for them, and re-layouts, transform(): return jnp.stack(blocks).astype(jnp.bfloat16)  18.3 us
    all_to_all x1, starting transfers between devices, shards(): lax.all_to_all(shaped, TA, split_axis=1, concat_axis=0, tiled=True)  15.9 us
    dot_general x7, matrix products, transform(): jnp.dot(kernel_rows, segment, preferred_element_type=jnp.float32)  11.7 us
    unnamed x20, local copies, waits for them, and re-layouts  10.8 us
  transfers between devices with their start and end apart: 1, of which 1 were waited for; matrix products, arithmetic and copies ran while one was open for 0% of the time, Pallas kernels for 0%

commit v1 on v0

v1 whole, which is shorter than its diff:
```python
import functools
import math

import jax
import jax.numpy as jnp
from jax import lax
from jax.experimental import pallas as pl
from jax.experimental.pallas import tpu as pltpu
from jax.sharding import Mesh
from jax.sharding import PartitionSpec as P

NFFT = 256
NB = 7
NF = 32
HALF = NB * NF
ROWS = 2 * HALF
TA = ("y", "zh", "x", "c")
F32 = jnp.float32
BF16 = jnp.bfloat16


def weights(block_starts, kept_freqs, times):
    offset = times[None, :] - block_starts[:, None]
    inside = (offset >= 0) & (offset < NFFT)
    window = 0.5 - 0.5 * jnp.cos(2.0 * math.pi / NFFT * offset.astype(F32))
    scale = jnp.where(inside, window, 0.0)
    phase = kept_freqs[None, :, None] * jnp.where(inside, offset, 0)[:, None, :] % NFFT
    angle = 2.0 * math.pi / NFFT * phase.astype(F32)
    norm = 2.0 / math.sqrt(NFFT)
    real = scale[:, None, :] * jnp.cos(angle) * norm
    imag = -scale[:, None, :] * jnp.sin(angle) * norm
    table = jnp.stack([real, imag]).astype(BF16)
    return table.reshape(ROWS, times.shape[0])


def same_freq(rows):
    row = lax.broadcasted_iota(jnp.int32, (rows, HALF), 0)
    col = lax.broadcasted_iota(jnp.int32, (rows, HALF), 1)
    return row % NF == col % NF


def dot(a, b):
    return jnp.dot(a, b, preferred_element_type=F32)


def dot_t(a, b):
    return lax.dot_general(a, b, (((1,), (1,)), ((), ())), preferred_element_type=F32)


def spectra_kernel(steps, w_ref, x_ref, s_ref, h_ref, acc):
    step = pl.program_id(0)
    parts = dot(w_ref[...], x_ref[...]).astype(BF16)
    for part in range(2):
        for b in range(NB):
            start = part * HALF + b * NF
            s_ref[b * 2 * NF + part * NF : b * 2 * NF + (part + 1) * NF, :] = parts[start : start + NF]
    real, imag = parts[:HALF], parts[HALF:]
    gram = dot_t(parts, real) + dot_t(jnp.concatenate([imag, -real], axis=0), imag)

    @pl.when(step == 0)
    def _():
        acc[...] = gram

    @pl.when(step > 0)
    def _():
        acc[...] += gram

    @pl.when(step == steps - 1)
    def _():
        kept = jnp.where(same_freq(ROWS), acc[...], 0.0)
        h_ref[...] = jnp.zeros_like(h_ref)
        h_ref[0 : 2 * NB, 0:HALF] = kept.reshape(2 * NB, NF, HALF).sum(axis=1)


def spectra_and_gram(w, x, width):
    times, pts = x.shape
    steps = pts // width
    return pl.pallas_call(
        functools.partial(spectra_kernel, steps),
        grid=(steps,),
        out_shape=(jax.ShapeDtypeStruct((ROWS, pts), BF16), jax.ShapeDtypeStruct((16, 256), F32)),
        in_specs=[
            pl.BlockSpec((ROWS, times), lambda i: (0, 0)),
            pl.BlockSpec((times, width), lambda i: (0, i)),
        ],
        out_specs=(pl.BlockSpec((ROWS, width), lambda i: (0, i)), pl.BlockSpec((16, 256), lambda i: (0, 0))),
        scratch_shapes=[pltpu.VMEM((ROWS, HALF), F32)],
        compiler_params=pltpu.CompilerParams(dimension_semantics=("arbitrary",), vmem_limit_bytes=40 * 2**20),
        cost_estimate=pl.CostEstimate(flops=2 * ROWS * times * pts, bytes_accessed=2 * times * pts, transcendentals=0),
        name="spectra",
    )(w, x)


def power_kernel(denominator, h_ref, s_ref, o_ref, m_ref):
    @pl.when(pl.program_id(0) == 0)
    def _():
        same = same_freq(NF)
        gram = h_ref[...] / denominator
        for b in range(NB):
            re = jnp.where(same, jnp.broadcast_to(gram[b : b + 1, :HALF], (NF, HALF)), 0.0)
            im = jnp.where(same, jnp.broadcast_to(gram[NB + b : NB + b + 1, :HALF], (NF, HALF)), 0.0)
            at = b * 2 * NF
            for part, (on_real, on_imag) in enumerate(((re, -im), (im, re))):
                for side, block in enumerate((on_real, on_imag)):
                    high = block.astype(BF16)
                    rows = slice(at + part * NF, at + (part + 1) * NF)
                    m_ref[2 * side, rows, :] = high
                    m_ref[2 * side + 1, rows, :] = (block - high.astype(F32)).astype(BF16)

    real = jnp.concatenate([s_ref[b * 2 * NF : b * 2 * NF + NF, :] for b in range(NB)], axis=0)
    imag = jnp.concatenate([s_ref[b * 2 * NF + NF : (b + 1) * 2 * NF, :] for b in range(NB)], axis=0)
    low = dot(m_ref[1], real) + dot(m_ref[3], imag)
    o_ref[...] = low + dot(m_ref[0], real) + dot(m_ref[2], imag)


def power(h, s, denominator, width):
    pts = s.shape[1]
    return pl.pallas_call(
        functools.partial(power_kernel, denominator),
        grid=(pts // width,),
        out_shape=jax.ShapeDtypeStruct((ROWS, pts), F32),
        in_specs=[pl.BlockSpec((16, 256), lambda i: (0, 0)), pl.BlockSpec((ROWS, width), lambda i: (0, i))],
        out_specs=pl.BlockSpec((ROWS, width), lambda i: (0, i)),
        scratch_shapes=[pltpu.VMEM((4, ROWS, HALF), BF16)],
        compiler_params=pltpu.CompilerParams(dimension_semantics=("arbitrary",), vmem_limit_bytes=40 * 2**20),
        name="power",
    )(h, s)


def sum_over(h, axes):
    count = lax.axis_size(axes)
    copies = jnp.broadcast_to(h[None], (count, *h.shape))
    return lax.all_to_all(copies, axes, 0, 0, tiled=True).sum(axis=0)


def shards(snapshots, block_starts, kept_freqs):
    count = lax.axis_size(TA)
    local = snapshots.shape[0]
    own = snapshots.shape[2] // count
    total = own * count * lax.axis_size("zl")
    blocks = snapshots.reshape(local, count, own).transpose(1, 0, 2)
    arrived = lax.all_to_all(blocks, TA, split_axis=0, concat_axis=0, tiled=True)
    w = weights(block_starts, kept_freqs, jnp.arange(local * count, dtype=jnp.int32))
    s, h = spectra_and_gram(w, arrived.reshape(local * count, own), 512)
    h = sum_over(h, ("y", "x"))
    h = sum_over(h, ("zh", "zl", "c"))
    out = power(h, s, float(NB * total), 512)
    shape = (1, NB, 2, NF, own)
    return s.reshape(shape), out.reshape(shape)


def solution(mesh):
    split = Mesh(mesh.devices.reshape(4, 2, 4, 2, mesh.shape["ga"]), ("y", "zh", "x", "c", "zl"))
    out = P("zl", None, None, None, TA)
    return jax.shard_map(
        shards, mesh=split, in_specs=(P(TA, "zl", None), P(), P()), out_specs=(out, out), check_vma=False
    )
```

time: 241 us -> 165 us (0.68)
  blocking collectives: 79.8 us -> 30.4 us
  local copies, waits for them, and re-layouts: 39.9 us -> 10.3 us
  waiting for transfers between devices: 68.2 us -> 91.4 us
  matrix products: 18.3 us -> 0 us
  between operations: 13.9 us -> 0.7 us
  Pallas kernels: 0 us -> 11.7 us
    psum x5 -> x0, blocking collectives: 79.8 us -> none  [one_axis_at_a_time(): x = lax.psum(x, axis)]
    all_to_all x0 -> x2, blocking collectives: none -> 30.4 us  [sum_over(): return lax.all_to_all(copies, axes, 0, 0, tiled=True).sum(axis=0)]
    all_to_all x1, waiting for transfers between devices: 68.2 us -> 91.4 us  [shards(): lax.all_to_all(blocks, TA, split_axis=0, concat_axis=0, tiled=True)]
    another operation x9 -> x0, local copies, waits for them, and re-layouts: 18.3 us -> none  [transform(): return jnp.stack(blocks).astype(jnp.bfloat16)]
    dot_general x15 -> x0, matrix products: 18.3 us -> none  [the longest x7 11.7 us: transform(): jnp.dot(kernel_rows, segment, preferred_element_type=jnp.float32)]
    pallas_call x0 -> x2, Pallas kernels: none -> 11.7 us  [the longest x1 7.74 us: spectra_and_gram(): pl.pallas_call(functools.partial(spectra_kernel, steps), grid=(steps,), o...]
    dot_general x4 -> x0, local copies, waits for them, and re-layouts: 5.59 us -> none  [the longest x1 1.63 us: gram_terms(): jnp.einsum('bfp,cfp->fbc', real_part, imag_part, preferred_element_type=f32)]
    unnamed x20 -> x7, local copies, waits for them, and re-layouts: 10.8 us -> 5.99 us
  transfers between devices with their start and end apart: 1 -> 1, of which waited for: 1 -> 1; matrix products, arithmetic and copies ran while one was open for 0% -> 3% of each run, Pallas kernels for 0% -> 0%
where the time goes in v1:
time: 165 us
  waiting for transfers between devices  91.4 us (55%)
  blocking collectives  30.4 us (18%)
  starting transfers between devices  15.9 us (10%)
  Pallas kernels  11.7 us (7%)
  local copies, waits for them, and re-layouts  10.3 us (6%)
  other arithmetic  4.36 us (3%)
    all_to_all x1, waiting for transfers between devices, shards(): lax.all_to_all(blocks, TA, split_axis=0, concat_axis=0, tiled=True)  91.4 us
    all_to_all x2, blocking collectives, sum_over(): return lax.all_to_all(copies, axes, 0, 0, tiled=True).sum(axis=0)  30.4 us
    all_to_all x1, starting transfers between devices, shards(): lax.all_to_all(blocks, TA, split_axis=0, concat_axis=0, tiled=True)  15.9 us
    pallas_call x1, Pallas kernels, spectra_and_gram(): pl.pallas_call(functools.partial(spectra_kernel, steps), grid=(steps,), o...  7.74 us
    unnamed x7, local copies, waits for them, and re-layouts  5.99 us
    reshape x1, local copies, waits for them, and re-layouts, shards(): blocks = snapshots.reshape(local, count, own).transpose(1, 0, 2)  4.27 us
    pallas_call x1, Pallas kernels, power(): pl.pallas_call(functools.partial(power_kernel, denominator), grid=(pts //...  3.99 us
    another operation x1, other arithmetic  3.95 us
  transfers between devices with their start and end apart: 1, of which 1 were waited for; matrix products, arithmetic and copies ran while one was open for 3% of the time, Pallas kernels for 0%

profile of v1, /device:TPU:1, one launch (start us, length us, event | category | flops | bytes accessed | tf_op | source)
XLA Modules:
  0.0 164.8 jit_solution(15309291800166218711)
XLA Ops:
  0.6 4.5 %copy.7 = bf16[2,8,64,2048]{3,2,1,0:T(8,128)(2,1)S(1)} copy(bf16[2,8,64,2048]{3,1,2,0:T(8,128)(2,1)} %bitcast.15) | data formatting | bytes 8388608
  5.1 4.3 %copy.9 = bf16[16,64,2048]{2,0,1:T(8,128)(2,1)} copy(bf16[16,64,2048]{2,1,0:T(8,128)(2,1)S(1)} %bitcast.14) | data formatting | bytes 8388608 | tf_op jit(solution)/shard_map/reshape | solution.py:141
  9.4 0.0 copy-start.1
  9.4 0.0 copy-start.2
  9.4 15.9 %all-to-all-start = ((bf16[64,16,2048]{2,1,0:T(8,128)(2,1)}), bf16[64,16,2048]{2,1,0:T(8,128)(2,1)}, u32[]{:S(2)}, u32[]{:S(2)}) async-start(bf16[64,16,2048]{2,1,0:T(8,128)(2,1)} %bitcast.13), calls=%async_computation | async-start | bytes 8388608 | tf_op jit(solution)/shard_map/all_to_all | solution.py:142
  25.3 0.0 copy-done.1
  25.3 0.1 fusion.3
  25.4 0.2 subtract_select_fusion
  25.6 0.0 copy-done.2
  25.6 3.9 %multiply_convert_fusion.1 = (bf16[1,7,32,1024]{3,2,1,0:T(8,128)(2,1)S(1)}, bf16[1,7,32,1024]{3,2,1,0:T(8,128)(2,1)S(1)}) fusion(s32[7,1024]{1,0:T(8,128)S(1)} %fusion.3, s32[32]{0:T(128)S(1)} %copy-done.2, f32[7,1024]{1,0:T(8,128)S(1)} %get-tuple-element.8, f32[7,1024]{1,0:T(8,128)S(1)} %get-tuple-element.9), kind=kLoop, calls=%fused_computation.11 | loop fusion | flops 4587520 | bytes 1003648 | tf_op jit(solution)/shard_map/convert
  29.6 0.1 pad_maximum_fusion
  29.7 91.4 %all-to-all-done = bf16[64,16,2048]{2,1,0:T(8,128)(2,1)} async-done(((bf16[64,16,2048]{2,1,0:T(8,128)(2,1)}), bf16[64,16,2048]{2,1,0:T(8,128)(2,1)}, u32[]{:S(2)}, u32[]{:S(2)}) %all-to-all-start) | async-done | bytes 4194336 | tf_op jit(solution)/shard_map/all_to_all | solution.py:142
  121.1 7.7 %spectra.1 = (bf16[448,2048]{1,0:T(8,128)(2,1)}, f32[16,256]{1,0:T(8,128)S(1)}) custom-call(bf16[448,1024]{1,0:T(8,128)(2,1)S(1)} %bitcast.12, bf16[1024,2048]{1,0:T(8,128)(2,1)} %bitcast.2.x_ref), custom_call_target="tpu_custom_call" | custom-call | flops 1879048192 | bytes 4194304 | tf_op jit(solution)/shard_map/spectra/pallas_call | solution.py:78
  128.9 14.8 %all_to_all.15 = f32[16,16,256]{2,1,0:T(8,128)S(1)} all-to-all(f32[16,16,256]{2,1,0:T(8,128)S(1)} %broadcast_in_dim.11), channel_id=1, replica_groups=mesh['y'=4,'zh'=2,'x'=4,'c'=2,'zl'=4] {'y','x'}, dimensions={0} | all-to-all | bytes 524288 | tf_op jit(solution)/shard_map/all_to_all | solution.py:133
  143.8 15.6 %all_to_all.16 = f32[16,16,256]{2,1,0:T(8,128)S(1)} all-to-all(f32[16,16,256]{2,1,0:T(8,128)S(1)} %broadcast_in_dim.12), channel_id=1, replica_groups=mesh['y'=4,'zh'=2,'x'=4,'c'=2,'zl'=4] {'zh','zl','c'}, dimensions={0} | all-to-all | bytes 524288 | tf_op jit(solution)/shard_map/all_to_all | solution.py:133
  159.4 0.0 copy-start
  159.4 1.5 copy-done
  160.9 4.0 %power.1 = f32[448,2048]{1,0:T(8,128)} custom-call(f32[16,256]{1,0:T(8,128)S(1)} %reduce_sum.19.h_ref, bf16[448,2048]{1,0:T(8,128)(2,1)S(1)} %copy-done), custom_call_target="tpu_custom_call" | custom-call | tf_op jit(solution)/shard_map/power/pallas_call | solution.py:118
  (4 shorter events, 0.1 us)
Async XLA Ops:
  9.4 15.9 %copy-start.1 = (s32[7]{0:T(128)S(1)}, s32[7]{0:T(128)}, u32[]{:S(2)}) copy-start(s32[7]{0:T(128)} %param.4) | copy-start | bytes 88
  9.4 16.2 %copy-start.2 = (s32[32]{0:T(128)S(1)}, s32[32]{0:T(128)}, u32[]{:S(2)}) copy-start(s32[32]{0:T(128)} %param.5) | copy-start | bytes 388
  9.4 111.7 %all-to-all-start = ((bf16[64,16,2048]{2,1,0:T(8,128)(2,1)}), bf16[64,16,2048]{2,1,0:T(8,128)(2,1)}, u32[]{:S(2)}, u32[]{:S(2)}) async-start(bf16[64,16,2048]{2,1,0:T(8,128)(2,1)} %bitcast.13), calls=%async_computation | async-start | bytes 8388608 | tf_op jit(solution)/shard_map/all_to_all | solution.py:142
  159.4 1.5 copy-start
